TPU v7x, 32 devices: a whole 2x2x4 slice. The times are simulated.
32 devices in a mesh: trial: 4 (over y, x), dp: 4 (over z), tp: 2 (over core).
Axes of the slice: x: 2, y: 2, z: 4, core: 2. Of those that a mesh axis runs over, the one named last changes fastest.
Arguments:
- slope_query: float32 [16, 768, 768], P(('trial', 'dp'), None, 'tp'), parts along dimension 0, may hold values from -4 to 4
- slope_key: float32 [16, 768, 768], P(('trial', 'dp'), None, 'tp'), parts along dimension 0, may hold values from -4 to 4
- slope_value: float32 [16, 768, 768], P(('trial', 'dp'), None, 'tp'), parts along dimension 0, may hold values from -4 to 4
- slope_mixed: float32 [16, 768, 768], P(('trial', 'dp'), 'tp'), parts along dimension 0, may hold values from -4 to 4
- slope_norm: float32 [16, 768], P(('trial', 'dp')), parts along dimension 0, may hold values from -8 to 8
- slope_bias: float32 [16, 768], P(('trial', 'dp')), parts along dimension 0, may hold values from -8 to 8
- param_query: float32 [3072, 768], P(('trial', 'dp'), 'tp'), parts along dimension 0, may hold values from -0.3125 to 0.3125
- param_key: float32 [3072, 768], P(('trial', 'dp'), 'tp'), parts along dimension 0, may hold values from -0.3125 to 0.3125
- param_value: float32 [3072, 768], P(('trial', 'dp'), 'tp'), parts along dimension 0, may hold values from -0.3125 to 0.3125
- param_mixed: float32 [3072, 768], P(('trial', 'tp'), 'dp'), parts along dimension 0, may hold values from -0.3125 to 0.3125
- param_norm: float32 [3072], P(('trial', 'dp')), parts along dimension 0, may hold values from 0.25 to 1.75
- param_bias: float32 [3072], P(('trial', 'dp')), parts along dimension 0, may hold values from -3 to 3
- state_query: float32 [3072, 768], P(('trial', 'dp'), 'tp'), parts along dimension 0, may hold values from 0.00026041668 to 0.0026041667
- state_key: float32 [3072, 768], P(('trial', 'dp'), 'tp'), parts along dimension 0, may hold values from 0.00026041668 to 0.0026041667
- state_value: float32 [3072, 768], P(('trial', 'dp'), 'tp'), parts along dimension 0, may hold values from 0.00026041668 to 0.0026041667
- state_mixed: float32 [3072, 768], P(('trial', 'tp'), 'dp'), parts along dimension 0, may hold values from 0.00026041668 to 0.0026041667
- state_norm: float32 [3072], P(('trial', 'dp')), parts along dimension 0, may hold values from 0.05 to 0.8
- state_bias: float32 [3072], P(('trial', 'dp')), parts along dimension 0, may hold values from 0.05 to 0.8
Outputs:
- half_query: bfloat16 [3072, 768], P('trial', 'tp'), parts along dimension 0
- half_key: bfloat16 [3072, 768], P('trial', 'tp'), parts along dimension 0
- half_value: bfloat16 [3072, 768], P('trial', 'tp'), parts along dimension 0
- half_mixed: bfloat16 [3072, 768], P(('trial', 'tp')), parts along dimension 0
- half_norm: bfloat16 [3072], P('trial'), parts along dimension 0
- half_bias: bfloat16 [3072], P('trial'), parts along dimension 0
- next_query: float32 [3072, 768], P(('trial', 'dp'), 'tp'), parts along dimension 0
- next_key: float32 [3072, 768], P(('trial', 'dp'), 'tp'), parts along dimension 0
- next_value: float32 [3072, 768], P(('trial', 'dp'), 'tp'), parts along dimension 0
- next_mixed: float32 [3072, 768], P(('trial', 'tp'), 'dp'), parts along dimension 0
- next_norm: float32 [3072], P(('trial', 'dp')), parts along dimension 0
- next_bias: float32 [3072], P(('trial', 'dp')), parts along dimension 0
- state_new_query: float32 [3072, 768], P(('trial', 'dp'), 'tp'), parts along dimension 0
- state_new_key: float32 [3072, 768], P(('trial', 'dp'), 'tp'), parts along dimension 0
- state_new_value: float32 [3072, 768], P(('trial', 'dp'), 'tp'), parts along dimension 0
- state_new_mixed: float32 [3072, 768], P(('trial', 'tp'), 'dp'), parts along dimension 0
- state_new_norm: float32 [3072], P(('trial', 'dp')), parts along dimension 0
- state_new_bias: float32 [3072], P(('trial', 'dp')), parts along dimension 0
There are 4 independent parts, one for each index of `trial`. A program takes and returns all parts, laid end to end along the dimension named above; each array names one. Nothing has to cross between parts.
All inputs are finite; a program needn't handle non-finite values.
Results may differ from a plain program's by a relative error of at most 0.001.
Values may be sent and summed in bfloat16 or wider, within the bound.
A program may use at most 64 MiB of HBM per device.

v0:
```python
import jax
import jax.numpy as jnp
from jax import lax
from jax.sharding import PartitionSpec as P

learn_rate = 0.02
hold_rate = 0.8


def shards(
    slope_query,
    slope_key,
    slope_value,
    slope_mixed,
    slope_norm,
    slope_bias,
    param_query,
    param_key,
    param_value,
    param_mixed,
    param_norm,
    param_bias,
    state_query,
    state_key,
    state_value,
    state_mixed,
    state_norm,
    state_bias,
):
    mean_query, mean_key, mean_value, mean_mixed = (
        lax.psum_scatter(slope_query[0], "dp", scatter_dimension=0, tiled=True),
        lax.psum_scatter(slope_key[0], "dp", scatter_dimension=0, tiled=True),
        lax.psum_scatter(slope_value[0], "dp", scatter_dimension=0, tiled=True),
        lax.psum_scatter(slope_mixed[0], "dp", scatter_dimension=1, tiled=True),
    )
    whole_norm, whole_bias = lax.psum((slope_norm[0], slope_bias[0]), "dp")
    place = lax.axis_index("dp")
    mean_norm = lax.dynamic_slice_in_dim(
        whole_norm, place * param_norm.shape[0], param_norm.shape[0]
    )
    mean_bias = lax.dynamic_slice_in_dim(
        whole_bias, place * param_bias.shape[0], param_bias.shape[0]
    )
    mean_rate = lax.axis_size("dp") ** (-0.5)
    mean_query = mean_query * mean_rate
    mean_key = mean_key * mean_rate
    mean_value = mean_value * mean_rate
    mean_mixed = mean_mixed * mean_rate
    mean_norm = mean_norm * mean_rate
    mean_bias = mean_bias * mean_rate
    (
        own_query,
        own_key,
        own_value,
        own_mixed,
        slope_query_norm,
        slope_key_norm,
        slope_value_norm,
        slope_mixed_norm,
    ) = lax.psum(
        (
            jnp.sum(param_query * param_query, axis=1, keepdims=True),
            jnp.sum(param_key * param_key, axis=1, keepdims=True),
            jnp.sum(param_value * param_value, axis=1, keepdims=True),
            jnp.sum(param_mixed * param_mixed, axis=0, keepdims=True),
            jnp.sum(mean_query * mean_query, axis=1, keepdims=True),
            jnp.sum(mean_key * mean_key, axis=1, keepdims=True),
            jnp.sum(mean_value * mean_value, axis=1, keepdims=True),
            jnp.sum(mean_mixed * mean_mixed, axis=0, keepdims=True),
        ),
        "tp",
    )
    mean_query = mean_query * (jnp.sqrt(own_query) * lax.rsqrt(slope_query_norm + 1e-06))
    mean_key = mean_key * (jnp.sqrt(own_key) * lax.rsqrt(slope_key_norm + 1e-06))
    mean_value = mean_value * (jnp.sqrt(own_value) * lax.rsqrt(slope_value_norm + 1e-06))
    mean_mixed = mean_mixed * (jnp.sqrt(own_mixed) * lax.rsqrt(slope_mixed_norm + 1e-06))
    state_new_query = hold_rate * state_query + (1.0 - hold_rate) * mean_query * mean_query
    next_query = param_query - learn_rate * mean_query * lax.rsqrt(state_new_query + 1e-06)
    state_new_key = hold_rate * state_key + (1.0 - hold_rate) * mean_key * mean_key
    next_key = param_key - learn_rate * mean_key * lax.rsqrt(state_new_key + 1e-06)
    state_new_value = hold_rate * state_value + (1.0 - hold_rate) * mean_value * mean_value
    next_value = param_value - learn_rate * mean_value * lax.rsqrt(state_new_value + 1e-06)
    state_new_mixed = hold_rate * state_mixed + (1.0 - hold_rate) * mean_mixed * mean_mixed
    next_mixed = param_mixed - learn_rate * mean_mixed * lax.rsqrt(state_new_mixed + 1e-06)
    state_new_norm = hold_rate * state_norm + (1.0 - hold_rate) * mean_norm * mean_norm
    next_norm = param_norm - learn_rate * mean_norm * lax.rsqrt(state_new_norm + 1e-06)
    state_new_bias = hold_rate * state_bias + (1.0 - hold_rate) * mean_bias * mean_bias
    next_bias = param_bias - learn_rate * mean_bias * lax.rsqrt(state_new_bias + 1e-06)
    half_query, half_key, half_value, half_mixed, half_norm, half_bias = (
        lax.all_gather(next_query.astype(jnp.bfloat16), "dp", axis=0, tiled=True),
        lax.all_gather(next_key.astype(jnp.bfloat16), "dp", axis=0, tiled=True),
        lax.all_gather(next_value.astype(jnp.bfloat16), "dp", axis=0, tiled=True),
        lax.all_gather(next_mixed.astype(jnp.bfloat16), "dp", axis=1, tiled=True),
        lax.all_gather(next_norm.astype(jnp.bfloat16), "dp", axis=0, tiled=True),
        lax.all_gather(next_bias.astype(jnp.bfloat16), "dp", axis=0, tiled=True),
    )
    return (
        half_query,
        half_key,
        half_value,
        half_mixed,
        half_norm,
        half_bias,
        next_query,
        next_key,
        next_value,
        next_mixed,
        next_norm,
        next_bias,
        state_new_query,
        state_new_key,
        state_new_value,
        state_new_mixed,
        state_new_norm,
        state_new_bias,
    )


def solution(mesh):
    in_specs = (
        P(("trial", "dp"), None, "tp"),
        P(("trial", "dp"), None, "tp"),
        P(("trial", "dp"), None, "tp"),
        P(("trial", "dp"), "tp", None),
        P(("trial", "dp"), None),
        P(("trial", "dp"), None),
        P(("trial", "dp"), "tp"),
        P(("trial", "dp"), "tp"),
        P(("trial", "dp"), "tp"),
        P(("trial", "tp"), "dp"),
        P(("trial", "dp")),
        P(("trial", "dp")),
        P(("trial", "dp"), "tp"),
        P(("trial", "dp"), "tp"),
        P(("trial", "dp"), "tp"),
        P(("trial", "tp"), "dp"),
        P(("trial", "dp")),
        P(("trial", "dp")),
    )
    out_specs = (
        P("trial", "tp"),
        P("trial", "tp"),
        P("trial", "tp"),
        P(("trial", "tp"), None),
        P("trial"),
        P("trial"),
        P(("trial", "dp"), "tp"),
        P(("trial", "dp"), "tp"),
        P(("trial", "dp"), "tp"),
        P(("trial", "tp"), "dp"),
        P(("trial", "dp")),
        P(("trial", "dp")),
        P(("trial", "dp"), "tp"),
        P(("trial", "dp"), "tp"),
        P(("trial", "dp"), "tp"),
        P(("trial", "tp"), "dp"),
        P(("trial", "dp")),
        P(("trial", "dp")),
    )
    return jax.shard_map(shards, mesh=mesh, in_specs=in_specs, out_specs=out_specs, check_vma=False)
```

profile of v0, /device:TPU:0, one launch (start us, length us, event | category | flops | bytes accessed | tf_op | source)
XLA Modules:
  0.0 215.3 jit_solution(6539019344068995075)
XLA Ops:
  7.2 0.0 reduce-scatter.5.cloned.1.call-start
  7.2 0.7 reduce-scatter.5.cloned.1.call-update
  7.9 0.0 reduce-scatter.7.cloned.1.call-start
  8.0 0.7 reduce-scatter.7.cloned.1.call-update
  8.7 0.0 reduce-scatter.9.cloned.1.call-start
  8.7 0.7 reduce-scatter.9.cloned.1.call-update
  9.4 0.0 reduce-scatter.11.cloned.1.call-start
  9.5 1.4 copy.38
  10.9 0.0 copy-start.16
  10.9 0.0 copy-start.17
  10.9 0.0 copy-start.18
  10.9 0.0 copy-start.1
  10.9 0.0 copy-start.2
  10.9 0.0 copy-start.3
  10.9 0.0 reduce-scatter.11.cloned.1.call-update
  11.0 0.6 copy-done.13
  11.6 0.6 dynamic-slice
  12.8 14.4 %all-reduce.2 = (f32[768]{0:T(1024)S(1)}, f32[768]{0:T(1024)S(1)}) all-reduce(f32[768]{0:T(1024)S(1)} %reduce, f32[768]{0:T(1024)S(1)} %reduce.1), channel_id=1, replica_groups=mesh['trial'=4,'dp'=4,'tp'=2] {'dp'}, use_global_device_ids=true, to_apply=%region_20.0 | all-reduce | flops 1536 | bytes 12288 | tf_op jit(solution)/shard_map/psum | solution.py:36
  27.3 0.7 fusion.4
  27.9 0.2 dynamic-update-slice
  28.1 0.2 dynamic-update-slice.1
  28.3 9.4 %all-reduce.4 = (bf16[768]{0:T(1024)(128)(2,1)}, bf16[768]{0:T(1024)(128)(2,1)}) all-reduce(bf16[768]{0:T(1024)(128)(2,1)S(1)} %dynamic-update-slice, bf16[768]{0:T(1024)(128)(2,1)S(1)} %dynamic-update-slice.1), channel_id=1, replica_groups=mesh['trial'=4,'dp'=4,'tp'=2] {'dp'}, use_global_device_ids=true, to_apply=%add | all-reduce | flops 1536 | bytes 6144
  37.8 0.1 multiply_reduce_fusion.7
  37.9 0.1 multiply_reduce_fusion.5
  38.0 0.1 multiply_reduce_fusion.3
  38.1 0.1 multiply_reduce_fusion.1
  38.3 4.6 %reduce-scatter.5.cloned.1.call-done = f32[192,384]{1,0:T(8,128)} async-done(((f32[768,384]{1,0:T(8,128)}), f32[192,384]{1,0:T(8,128)}) %reduce-scatter.5.cloned.1.call-update) | async-done | bytes 294928 | tf_op jit(solution)/shard_map/reduce_scatter | solution.py:31
  42.8 1.1 multiply_reduce_fusion.6
  44.0 29.4 %reduce-scatter.7.cloned.1.call-done = f32[192,384]{1,0:T(8,128)} async-done(((f32[768,384]{1,0:T(8,128)}), f32[192,384]{1,0:T(8,128)}) %reduce-scatter.7.cloned.1.call-update) | async-done | bytes 294928 | tf_op jit(solution)/shard_map/reduce_scatter | solution.py:32
  73.4 1.1 multiply_reduce_fusion.4
  74.4 29.2 %reduce-scatter.9.cloned.1.call-done = f32[192,384]{1,0:T(8,128)} async-done(((f32[768,384]{1,0:T(8,128)}), f32[192,384]{1,0:T(8,128)}) %reduce-scatter.9.cloned.1.call-update) | async-done | bytes 294928 | tf_op jit(solution)/shard_map/reduce_scatter | solution.py:33
  103.6 1.1 multiply_reduce_fusion.2
  104.7 29.0 %reduce-scatter.11.cloned.1.call-done = f32[384,192]{0,1:T(8,128)} async-done(((f32[384,768]{0,1:T(8,128)}), f32[384,192]{0,1:T(8,128)}) %reduce-scatter.11.cloned.1.call-update) | async-done | bytes 294928 | tf_op jit(solution)/shard_map/reduce_scatter | solution.py:34
  133.8 1.1 multiply_reduce_fusion
  134.8 2.5 %all-reduce.3 = (f32[192,1]{0,1:T(1,128)S(1)}, f32[192,1]{0,1:T(1,128)S(1)}, f32[192,1]{0,1:T(1,128)S(1)}, f32[192,1]{0,1:T(1,128)S(1)}, f32[192,1]{0,1:T(1,128)...) all-reduce(f32[192,1]{0,1:T(1,128)S(1)} %bitcast.25, ...), channel_id=1, replica_groups=mesh['trial'=4,'dp'=4,'tp'=2] {'tp'}, use_global_device_ids=true, to_apply=%region_4.0 | all-reduce | flops 1536 | bytes 12288 | tf_op jit(solution)/shard_map/psum | solution.py:60
  137.4 0.0 copy-start.10
  137.4 1.0 fusion.12
  138.4 16.6 %all_gather.18 = bf16[768,384]{1,0:T(8,128)(2,1)S(1)} all-gather(bf16[192,384]{1,0:T(8,128)(2,1)S(1)} %get-tuple-element.81), channel_id=1, replica_groups=mesh['trial'=4,'dp'=4,'tp'=2] {'dp'}, dimensions={0}, use_global_device_ids=true | all-gather | bytes 737280 | tf_op jit(solution)/shard_map/all_gather | solution.py:90
  155.0 1.0 fusion.10
  156.0 16.1 %all_gather.19 = bf16[768,384]{1,0:T(8,128)(2,1)S(1)} all-gather(bf16[192,384]{1,0:T(8,128)(2,1)S(1)} %get-tuple-element.78), channel_id=1, replica_groups=mesh['trial'=4,'dp'=4,'tp'=2] {'dp'}, dimensions={0}, use_global_device_ids=true | all-gather | bytes 737280 | tf_op jit(solution)/shard_map/all_gather | solution.py:91
  172.1 1.0 fusion.8
  173.1 16.2 %all_gather.20 = bf16[768,384]{1,0:T(8,128)(2,1)S(1)} all-gather(bf16[192,384]{1,0:T(8,128)(2,1)S(1)} %get-tuple-element.75), channel_id=1, replica_groups=mesh['trial'=4,'dp'=4,'tp'=2] {'dp'}, dimensions={0}, use_global_device_ids=true | all-gather | bytes 737280 | tf_op jit(solution)/shard_map/all_gather | solution.py:92
  189.3 1.0 fusion.6
  190.3 14.9 %all_gather.21 = bf16[384,768]{0,1:T(8,128)(2,1)S(1)} all-gather(bf16[384,192]{0,1:T(8,128)(2,1)S(1)} %get-tuple-element.72), channel_id=1, replica_groups=mesh['trial'=4,'dp'=4,'tp'=2] {'dp'}, dimensions={1}, use_global_device_ids=true | all-gather | bytes 737280 | tf_op jit(solution)/shard_map/all_gather | solution.py:93
  205.2 1.1 copy.39
  206.3 0.8 copy.45
  207.1 0.8 copy.46
  207.9 0.8 copy.47
  (39 shorter events, 0.1 us)
Async XLA Ops:
  7.2 35.6 %reduce-scatter.5.cloned.1.call-start = ((), (), s32[]{:S(2)}) async-start(), calls=%async_computation.4 | async-start | bytes 1474560 | tf_op jit(solution)/shard_map/reduce_scatter | solution.py:31
  7.9 65.4 %reduce-scatter.7.cloned.1.call-start = ((), (), s32[]{:S(2)}) async-start(), calls=%async_computation.5 | async-start | bytes 1474560 | tf_op jit(solution)/shard_map/reduce_scatter | solution.py:32
  8.0 1.5 copy-start
  8.7 95.0 %reduce-scatter.9.cloned.1.call-start = ((), (), s32[]{:S(2)}) async-start(), calls=%async_computation.6 | async-start | bytes 1474560 | tf_op jit(solution)/shard_map/reduce_scatter | solution.py:33
  9.4 124.4 %reduce-scatter.11.cloned.1.call-start = ((), (), s32[]{:S(2)}) async-start(), calls=%async_computation.7 | async-start | bytes 1474560 | tf_op jit(solution)/shard_map/reduce_scatter | solution.py:34
  10.8 0.7 copy-start.13
  10.8 0.7 copy-start.14
  10.8 0.7 copy-start.19
  10.8 16.4 %copy-start.15 = (f32[192]{0:T(256)S(1)}, f32[192]{0:T(256)}, u32[]{:S(2)}) copy-start(f32[192]{0:T(256)} %param.29) | copy-start | bytes 2308
  10.9 16.4 %copy-start.16 = (f32[192]{0:T(256)S(1)}, f32[192]{0:T(256)}, u32[]{:S(2)}) copy-start(f32[192]{0:T(256)} %param.35) | copy-start | bytes 2308
  10.9 16.4 %copy-start.17 = (f32[192]{0:T(256)S(1)}, f32[192]{0:T(256)}, u32[]{:S(2)}) copy-start(f32[192]{0:T(256)} %param.28) | copy-start | bytes 2308
  10.9 16.4 %copy-start.18 = (f32[192]{0:T(256)S(1)}, f32[192]{0:T(256)}, u32[]{:S(2)}) copy-start(f32[192]{0:T(256)} %param.34) | copy-start | bytes 2308
  10.9 26.9 %copy-start.1 = (f32[192,384]{1,0:T(8,128)S(1)}, f32[192,384]{1,0:T(8,128)}, u32[]{:S(2)}) copy-start(f32[192,384]{1,0:T(8,128)} %param.24) | copy-start | bytes 884740
  10.9 27.0 %copy-start.2 = (f32[192,384]{1,0:T(8,128)S(1)}, f32[192,384]{1,0:T(8,128)}, u32[]{:S(2)}) copy-start(f32[192,384]{1,0:T(8,128)} %param.25) | copy-start | bytes 884740
  10.9 27.1 %copy-start.3 = (f32[192,384]{1,0:T(8,128)S(1)}, f32[192,384]{1,0:T(8,128)}, u32[]{:S(2)}) copy-start(f32[192,384]{1,0:T(8,128)} %param.26) | copy-start | bytes 884740
  10.9 27.2 %copy-start.4 = (f32[384,192]{0,1:T(8,128)S(1)}, f32[384,192]{0,1:T(8,128)}, u32[]{:S(2)}) copy-start(f32[384,192]{0,1:T(8,128)} %param.27) | copy-start | bytes 884740
  37.8 99.6 %copy-start.9 = (f32[192,384]{1,0:T(8,128)S(1)}, f32[192,384]{1,0:T(8,128)}, u32[]{:S(2)}) copy-start(f32[192,384]{1,0:T(8,128)} %param.30) | copy-start | bytes 884740
  42.8 94.5 %copy-start.8 = (f32[192,384]{1,0:T(8,128)S(1)}, f32[192,384]{1,0:T(8,128)}, u32[]{:S(2)}) copy-start(f32[192,384]{1,0:T(8,128)} %reduce-scatter.5.cloned.1.call-done) | copy-start | bytes 884740
  137.4 17.6 %copy-start.5 = (f32[192,384]{1,0:T(8,128)S(1)}, f32[192,384]{1,0:T(8,128)}, u32[]{:S(2)}) copy-start(f32[192,384]{1,0:T(8,128)} %reduce-scatter.7.cloned.1.call-done) | copy-start | bytes 884740
  137.4 17.6 %copy-start.10 = (f32[192,384]{1,0:T(8,128)S(1)}, f32[192,384]{1,0:T(8,128)}, u32[]{:S(2)}) copy-start(f32[192,384]{1,0:T(8,128)} %param.31) | copy-start | bytes 884740
  155.0 17.1 %copy-start.7 = (f32[192,384]{1,0:T(8,128)S(1)}, f32[192,384]{1,0:T(8,128)}, u32[]{:S(2)}) copy-start(f32[192,384]{1,0:T(8,128)} %reduce-scatter.9.cloned.1.call-done) | copy-start | bytes 884740
  155.0 17.1 %copy-start.11 = (f32[192,384]{1,0:T(8,128)S(1)}, f32[192,384]{1,0:T(8,128)}, u32[]{:S(2)}) copy-start(f32[192,384]{1,0:T(8,128)} %param.32) | copy-start | bytes 884740
  172.1 17.2 %copy-start.6 = (f32[384,192]{0,1:T(8,128)S(1)}, f32[384,192]{0,1:T(8,128)}, u32[]{:S(2)}) copy-start(f32[384,192]{0,1:T(8,128)} %reduce-scatter.11.cloned.1.call-done) | copy-start | bytes 884740
  172.1 17.2 %copy-start.12 = (f32[384,192]{0,1:T(8,128)S(1)}, f32[384,192]{0,1:T(8,128)}, u32[]{:S(2)}) copy-start(f32[384,192]{0,1:T(8,128)} %param.33) | copy-start | bytes 884740
Sparse Core Ops, SparseCore 0:
  10.3 32.4 reduce-scatter.4
  45.1 28.1 reduce-scatter.6
  75.7 27.9 reduce-scatter.8
  105.8 27.9 reduce-scatter.10
where the time goes:
time: 216 us; the launch traced here: 215 us
  waiting for transfers between devices  94.3 us (44%)
  blocking collectives  90.1 us (42%)
  between operations  14.8 us (7%)
  other arithmetic  9.46 us (4%)
  local copies, waits for them, and re-layouts  6.54 us (3%)
    reduce_scatter x1, waiting for transfers between devices, shards(): lax.psum_scatter(slope_key[0], 'dp', scatter_dimension=0, tiled=True)  29.4 us
    reduce_scatter x1, waiting for transfers between devices, shards(): lax.psum_scatter(slope_value[0], 'dp', scatter_dimension=0, tiled=True)  29.2 us
    reduce_scatter x1, waiting for transfers between devices, shards(): lax.psum_scatter(slope_mixed[0], 'dp', scatter_dimension=1, tiled=True)  29 us
    all_gather x1, blocking collectives, shards(): lax.all_gather(next_query.astype(jnp.bfloat16), 'dp', axis=0, tiled=True)  16.6 us
    all_gather x1, blocking collectives, shards(): lax.all_gather(next_value.astype(jnp.bfloat16), 'dp', axis=0, tiled=True)  16.2 us
    all_gather x1, blocking collectives, shards(): lax.all_gather(next_key.astype(jnp.bfloat16), 'dp', axis=0, tiled=True)  16.1 us
    all_gather x1, blocking collectives, shards(): lax.all_gather(next_mixed.astype(jnp.bfloat16), 'dp', axis=1, tiled=True)  14.9 us
    psum x1, blocking collectives, shards(): whole_norm, whole_bias = lax.psum((slope_norm[0], slope_bias[0]), 'dp')  14.4 us
  transfers between devices with their start and end apart: 4, of which 4 were waited for; matrix products, arithmetic and copies ran while one was open for 3% of the time, Pallas kernels for 0%

commit v1 on v0

--- a/solution.py
+++ b/solution.py
@@ -1,6 +1,10 @@
+import functools
+
 import jax
 import jax.numpy as jnp
 from jax import lax
+from jax.experimental import pallas as pl
+from jax.experimental.pallas import tpu as pltpu
 from jax.sharding import PartitionSpec as P
 
 learn_rate = 0.02
@@ -116,6 +120,401 @@
     )
 
 
+MESH = pl.DeviceIdType.MESH
+HALVES = 2
+GAIN = 1024.0
+ORDER = (0, 3, 1, 2)
+
+
+def plan_of(mesh):
+    n, pair = mesh.shape["dp"], mesh.shape["tp"]
+    return n if pair == 2 and n == 4 else None
+
+
+def encode(x):
+    t = x * GAIN
+    t = t * t
+    t = t * t
+    t = t * t
+    return jnp.where(x < 0, -t, t).astype(jnp.bfloat16)
+
+
+def decode(y):
+    y = y.astype(jnp.float32)
+    fourth = lax.rsqrt(lax.rsqrt(jnp.abs(y)))
+    root = fourth * lax.rsqrt(jnp.maximum(fourth, 1e-30)) * (1.0 / GAIN)
+    return jnp.where(y < 0, -root, root)
+
+
+def update(param, state, mean):
+    state_new = hold_rate * state + (1.0 - hold_rate) * mean * mean
+    return state_new, param - learn_rate * mean * lax.rsqrt(state_new + 1e-06)
+
+
+def kernel(n, *refs):
+    (sq, sk, sv, sm, sn, sb, pq, pk, pv, pm, pn, pb, tq, tk, tv, tm, tn, tb) = refs[:18]
+    (hq, hk, hv, hm, hn, hb, xq, xk, xv, xm, xn, xb, nq, nk, nv, nm, nn, nb) = refs[18:36]
+    (X, XM, S, RL, RR, G, P_, T_, PM, TM, NX, NS, TOT, ES, ER, HM, VB, VR, NV,
+     load_sem, mix_sem, par_sem, rs_send, rl_sem, rr_sem, ag_send, ag_send2, ag_recv,
+     e_send, e_recv, v_send, v_recv, out_sem, half_sem) = refs[36:]
+    C, _, B, W = X.shape
+    H = HALVES
+    own = B * H
+    mixc = H * ORDER.index(3)
+    me = lax.axis_index("dp")
+    core = lax.axis_index("tp")
+    rate = float(n) ** (-0.5)
+    slopes = (sq, sk, sv)
+    order = [n - 1, 0] + [j for j in range(n - 2, 0, -1)]
+
+    loads = [None] * C
+    for at, m in enumerate(ORDER):
+        if m < 3:
+            for h in range(H):
+                c = at * H + h
+                loads[c] = pltpu.make_async_copy(slopes[m].at[:, h], X.at[c], load_sem.at[c])
+                loads[c].start()
+        else:
+            mix = pltpu.make_async_copy(sm, XM, mix_sem)
+            mix.start()
+    pars = []
+    for at, m in enumerate(ORDER):
+        for k, (srcs, dst, odd) in enumerate((((pq, pk, pv, pm), P_, PM), ((tq, tk, tv, tm), T_, TM))):
+            d = odd if m == 3 else dst.at[pl.ds(at * H, H)]
+            cp = pltpu.make_async_copy(srcs[m], d, par_sem.at[k, m])
+            cp.start()
+            pars.append(cp)
+
+    barrier = pltpu.get_barrier_semaphore()
+    for d in range(1, n):
+        pl.semaphore_signal(barrier, inc=1, device_id={"dp": lax.rem(me + d, n)}, device_id_type=MESH)
+    pl.semaphore_signal(barrier, inc=1, device_id={"tp": 1 - core}, device_id_type=MESH)
+
+    part = sn.shape[1] // n
+    for j in range(n):
+        VB[j : j + 1, :part] = sn[:, j * part : (j + 1) * part]
+        VB[n + j : n + j + 1, :part] = sb[:, j * part : (j + 1) * part]
+    for k, r in enumerate((pn, pb, tn, tb)):
+        VB[2 * n + k : 2 * n + k + 1, :part] = r[...]
+    pl.semaphore_wait(barrier, n)
+
+    def hop(src, dst, ss, rs, to):
+        return pltpu.make_async_remote_copy(
+            src_ref=src, dst_ref=dst, send_sem=ss, recv_sem=rs, device_id={"dp": to}, device_id_type=MESH
+        )
+
+    right, left = jnp.minimum(me + 1, n - 1), jnp.maximum(me - 1, 0)
+
+    def rs_right(c, j):
+        return hop(S.at[c, j], RL.at[c, j], rs_send.at[c, j], rl_sem.at[c, j], right)
+
+    def rs_left(c, j):
+        return hop(S.at[c, j], RR.at[c, j], rs_send.at[c, j], rr_sem.at[c, j], left)
+
+    def ag_right(c, j):
+        return hop(G.at[c, j], G.at[c, j], ag_send.at[c, j], ag_recv.at[c, j], right)
+
+    def ag_left(c, j):
+        return hop(G.at[c, j], G.at[c, j], ag_send.at[c, j], ag_recv.at[c, j], left)
+
+    def ag_left_own(c):
+        return hop(G.at[c, me], G.at[c, me], ag_send2.at[c], ag_recv.at[c, me], left)
+
+    def vec(d):
+        return hop(VB, VR.at[n - d], v_send.at[d], v_recv.at[n - d], lax.rem(me + d, n))
+
+    def pair(c):
+        return pltpu.make_async_remote_copy(
+            src_ref=ES.at[c], dst_ref=ER.at[c], send_sem=e_send.at[c], recv_sem=e_recv.at[c],
+            device_id={"tp": 1 - core}, device_id_type=MESH,
+        )
+
+    def rs(c):
+        for j in order:
+            for go, first, wait, land, send in (
+                (me < j, me == 0, rs_right, RL, rs_right),
+                (me > j, me == n - 1, rs_left, RR, rs_left),
+            ):
+                @pl.when(go)
+                def _(j=j, first=first, wait=wait, land=land, send=send):
+                    @pl.when(first)
+                    def _():
+                        S[c, j] = encode(X[c, j])
+
+                    @pl.when(jnp.logical_not(first))
+                    def _():
+                        wait(c, j).wait_recv()
+                        S[c, j] = encode(decode(land[c, j]) + X[c, j])
+
+                    send(c, j).start()
+
+    def gather_sum(c):
+        TOT[c] = X[c, me]
+
+        @pl.when(me > 0)
+        def _():
+            rs_right(c, me).wait_recv()
+            TOT[c] = TOT[c] + decode(RL[c, me])
+
+        @pl.when(me < n - 1)
+        def _():
+            rs_left(c, me).wait_recv()
+            TOT[c] = TOT[c] + decode(RR[c, me])
+
+        mean = TOT[c] * rate
+        TOT[c] = mean
+        p = P_[c]
+        lane = lax.broadcasted_iota(jnp.int32, (B, 128), 1)
+        ES[c] = jnp.where(
+            lane < 64, jnp.sum(p * p, axis=1, keepdims=True), jnp.sum(mean * mean, axis=1, keepdims=True)
+        )
+        pair(c).start()
+
+    def apply(c):
+        pair(c).wait_recv()
+        both = ES[c] + ER[c]
+        ratio = jnp.sqrt(both[:, :1]) * lax.rsqrt(both[:, 64:65] + 1e-06)
+        state_new, nxt = update(P_[c], T_[c], TOT[c] * ratio)
+        G[c, me] = nxt.astype(jnp.bfloat16)
+        NX[c] = nxt
+        NS[c] = state_new
+
+        @pl.when(me < n - 1)
+        def _():
+            ag_right(c, me).start()
+
+        @pl.when(me > 0)
+        def _():
+            ag_left_own(c).start()
+
+    def passes(j):
+        return jnp.logical_or(
+            jnp.logical_and(me > j, me < n - 1), jnp.logical_and(me < j, me > 0)
+        )
+
+    def take(c, j):
+        ag_right(c, j).wait_recv()
+
+        @pl.when(jnp.logical_and(me > j, me < n - 1))
+        def _():
+            ag_right(c, j).start()
+
+        @pl.when(jnp.logical_and(me < j, me > 0))
+        def _():
+            ag_left(c, j).start()
+
+    def mixed_in():
+        mix.wait()
+        for b in range(XM.shape[1] // 128):
+            t = XM[:, b * 128 : b * 128 + 128].T
+            for p in range(4):
+                r = b * 128 + p * 32
+                X[mixc + (r % own) // B, r // own, r % B : r % B + 32] = t[p * 32 : p * 32 + 32]
+        for src, dst in ((PM, P_), (TM, T_)):
+            t = src[...].T
+            for h in range(H):
+                dst[mixc + h] = t[h * B : h * B + B]
+
+    for d in range(1, n):
+        vec(d).start()
+    for c in range(C):
+        if loads[c] is not None and c < H:
+            loads[c].wait()
+    VR[0] = VB[...]
+    for c in range(H):
+        rs(c)
+    for c in range(C):
+        if loads[c] is not None and c >= H:
+            loads[c].wait()
+    for cp in pars:
+        cp.wait()
+    mixed_in()
+
+    def step(t, carry):
+        @pl.when(t < C)
+        def _():
+            rs(t)
+
+        @pl.when(jnp.logical_and(t >= 1, t <= C))
+        def _():
+            gather_sum(t - 1)
+
+        @pl.when(jnp.logical_and(t >= 2, t <= C + 1))
+        def _():
+            apply(t - 2)
+
+        @pl.when(t >= 3)
+        def _():
+            for j in range(1, n - 1):
+                @pl.when(passes(j))
+                def _(j=j):
+                    take(t - 3, j)
+
+        return carry
+
+    gather_sum(0)
+    lax.fori_loop(H, C + 3, step, 0)
+
+    nexts, news = (xq, xk, xv), (nq, nk, nv)
+    outs = []
+    for at, m in enumerate(ORDER):
+        for k, (buf, dsts, odd, mo) in enumerate(((NX, nexts, PM, xm), (NS, news, TM, nm))):
+            if m < 3:
+                cp = pltpu.make_async_copy(buf.at[pl.ds(at * H, H)], dsts[m], out_sem.at[k, m])
+            else:
+                odd[...] = jnp.concatenate([buf[mixc + h] for h in range(H)], axis=0).T
+                cp = pltpu.make_async_copy(odd, mo, out_sem.at[k, m])
+            cp.start()
+            outs.append(cp)
+
+    for d in range(1, n):
+        vec(d).wait_send()
+        vec(n - d).wait_recv()
+    total = VR[0, : 2 * n]
+    for d in range(1, n):
+        total = total + VR[d, : 2 * n]
+    NV[0] = total * rate
+    for d in range(n):
+        at = lax.rem(me + d, n)
+        for k in range(2):
+            mean = NV[0, pl.ds(k * n + at, 1), :]
+            state_new, nxt = update(
+                VR[d, 2 * n + k : 2 * n + k + 1], VR[d, 2 * n + 2 + k : 2 * n + 3 + k], mean
+            )
+            NV[1, pl.ds(k * n + at, 1), :] = nxt
+            if d == 0:
+                (xn, xb)[k][...] = nxt[:, :part]
+                (nn, nb)[k][...] = state_new[:, :part]
+    for k, o in enumerate((hn, hb)):
+        o[...] = jnp.concatenate(
+            [NV[1, k * n + j : k * n + j + 1, :part] for j in range(n)], axis=1
+        ).astype(jnp.bfloat16)
+
+    halves = (hq, hk, hv)
+
+    def finish(c):
+        for j in range(n):
+            open_ = me != j
+            if 0 < j < n - 1:
+                open_ = jnp.logical_and(open_, jnp.logical_not(passes(j)))
+
+            @pl.when(open_)
+            def _(j=j):
+                take(c, j)
+
+    stores = []
+    for at, m in enumerate(ORDER):
+        for h in range(H):
+            c = at * H + h
+            finish(c)
+            if m < 3:
+                cp = pltpu.make_async_copy(G.at[c], halves[m].at[:, h], half_sem.at[c])
+                cp.start()
+                stores.append(cp)
+        if m == 3:
+            for j in range(n // 2):
+                rows = [G[at * H + h, 2 * j + i].astype(jnp.float32) for i in range(2) for h in range(H)]
+                HM[:, j * 2 * own : (j + 1) * 2 * own] = jnp.concatenate(rows, axis=0).T.astype(jnp.bfloat16)
+            cp = pltpu.make_async_copy(HM, hm, half_sem.at[at * H])
+            cp.start()
+            stores.append(cp)
+
+    def drain(c, carry):
+        for j in range(n):
+            @pl.when(me != j)
+            def _(j=j):
+                rs_right(c, j).wait_send()
+
+            @pl.when(jnp.logical_and(me != j, passes(j)))
+            def _(j=j):
+                ag_right(c, j).wait_send()
+
+        @pl.when(me < n - 1)
+        def _():
+            ag_right(c, me).wait_send()
+
+        @pl.when(me > 0)
+        def _():
+            ag_left_own(c).wait_send()
+
+        pair(c).wait_send()
+        return carry
+
+    lax.fori_loop(0, C, drain, 0)
+    for cp in outs + stores:
+        cp.wait()
+
+
+def fused(n, *args):
+    slopes, params, states = list(args[:6]), list(args[6:12]), list(args[12:])
+    own, width = params[0].shape
+    H = HALVES
+    B = own // H
+    if own % (H * 32) or width % 128 or args[3].shape[1:] != (width, n * own) or args[3].shape[2] % 256:
+        return shards(*args)
+    C = H * 4
+    for i in range(3):
+        slopes[i] = slopes[i].reshape(n, H, B, width)
+        params[i] = params[i].reshape(H, B, width)
+        states[i] = states[i].reshape(H, B, width)
+    slopes[3] = slopes[3][0]
+    for group in (params, states):
+        for i in (4, 5):
+            group[i] = group[i].reshape(1, -1)
+    any_, vmem = pl.BlockSpec(memory_space=pl.ANY), pl.BlockSpec(memory_space=pltpu.VMEM)
+    f32, bf16 = jnp.float32, jnp.bfloat16
+    specs = [any_] * 4 + [vmem] * 2
+    S = jax.ShapeDtypeStruct
+    rows = n * own
+    shape = (
+        [S((n, H, B, width), bf16)] * 3 + [S((width, rows), bf16)] + [S((1, rows), bf16)] * 2
+        + ([S((H, B, width), f32)] * 3 + [S((width, own), f32)] + [S((1, own), f32)] * 2) * 2
+    )
+    wide = -(-own // 128) * 128
+    dma = pltpu.SemaphoreType.DMA
+    outs = pl.pallas_call(
+        functools.partial(kernel, n),
+        out_shape=shape,
+        in_specs=specs * 3,
+        out_specs=specs * 3,
+        scratch_shapes=[
+            pltpu.VMEM((C, n, B, width), f32),
+            pltpu.VMEM((width, rows), f32),
+            pltpu.VMEM((C, n, B, width), bf16),
+            pltpu.VMEM((C, n, B, width), bf16),
+            pltpu.VMEM((C, n, B, width), bf16),
+            pltpu.VMEM((C, n, B, width), bf16),
+            pltpu.VMEM((C, B, width), f32),
+            pltpu.VMEM((C, B, width), f32),
+            pltpu.VMEM((width, own), f32),
+            pltpu.VMEM((width, own), f32),
+            pltpu.VMEM((C, B, width), f32),
+            pltpu.VMEM((C, B, width), f32),
+            pltpu.VMEM((C, B, width), f32),
+            pltpu.VMEM((C, B, 128), f32),
+            pltpu.VMEM((C, B, 128), f32),
+            pltpu.VMEM((width, rows), bf16),
+            pltpu.VMEM((16, wide), f32),
+            pltpu.VMEM((n, 16, wide), f32),
+            pltpu.VMEM((2, 2 * n, wide), f32),
+            dma((C,)), dma, dma((2, 4)), dma((C, n)), dma((C, n)), dma((C, n)), dma((C, n)), dma((C,)), dma((C, n)),
+            dma((C,)), dma((C,)), dma((n,)), dma((n,)), dma((2, 4)), dma((C,)),
+        ],
+        compiler_params=pltpu.CompilerParams(
+            collective_id=0, has_side_effects=True, vmem_limit_bytes=48 * 2**20
+        ),
+        cost_estimate=pl.CostEstimate(flops=10**7, bytes_accessed=10**7, transcendentals=0),
+    )(*slopes, *params, *states)
+    outs = list(outs)
+    for i in range(3):
+        outs[i] = outs[i].reshape(rows, width)
+        for k in (6, 12):
+            outs[k + i] = outs[k + i].reshape(own, width)
+    for k in (4, 5, 10, 11, 16, 17):
+        outs[k] = outs[k].reshape(-1)
+    return tuple(outs)
+
+
 def solution(mesh):
     in_specs = (
         P(("trial", "dp"), None, "tp"),
@@ -157,4 +556,6 @@
         P(("trial", "dp")),
         P(("trial", "dp")),
     )
-    return jax.shard_map(shards, mesh=mesh, in_specs=in_specs, out_specs=out_specs, check_vma=False)
+    plan = plan_of(mesh)
+    body = shards if plan is None else functools.partial(fused, plan)
+    return jax.shard_map(body, mesh=mesh, in_specs=in_specs, out_specs=out_specs, check_vma=False)

time: 216 us -> 183 us (0.85)
  Pallas kernels: 0 us -> 160 us
  waiting for transfers between devices: 94.3 us -> 0 us
  blocking collectives: 90.1 us -> 0 us
  between operations: 14.8 us -> 0.88 us
  local copies, waits for them, and re-layouts: 6.54 us -> 20.2 us
  other arithmetic: 9.46 us -> 1.19 us
    pallas_call x0 -> x1, Pallas kernels: none -> 160 us  [fused(): pl.pallas_call(functools.partial(kernel, n), out_shape=shape, in_specs=sp...]
    reduce_scatter x4 -> x0, waiting for transfers between devices: 92.2 us -> none  [the longest x1 29.4 us: shards(): lax.psum_scatter(slope_key[0], 'dp', scatter_dimension=0, tiled=True)]
    all_gather x4 -> x0, blocking collectives: 63.8 us -> none  [the longest x1 16.6 us: shards(): lax.all_gather(next_query.astype(jnp.bfloat16), 'dp', axis=0, tiled=True)]
    psum x2 -> x0, blocking collectives: 16.9 us -> none  [the longest x1 14.4 us: shards(): whole_norm, whole_bias = lax.psum((slope_norm[0], slope_bias[0]), 'dp')]
    unnamed x50 -> x72, local copies, waits for them, and re-layouts: 6.54 us -> 20.2 us
    unnamed x1 -> x0, blocking collectives: 9.43 us -> none
    reduce_sum x8 -> x0, other arithmetic: 4.82 us -> none  [the longest x1 1.15 us: shards(): jnp.sum(mean_query * mean_query, axis=1, keepdims=True)]
    convert_element_type x5 -> x0, other arithmetic: 4.57 us -> none  [the longest x1 0.98 us: shards(): next_query.astype(jnp.bfloat16)]
  transfers between devices with their start and end apart: 4 -> 0, of which waited for: 4 -> 0; matrix products, arithmetic and copies ran while one was open for 3% -> 0% of each run, Pallas kernels for 0% -> 0%
where the time goes in v1:
time: 183 us; the launch traced here: 182 us
  Pallas kernels  160 us (87%)
  local copies, waits for them, and re-layouts  20.2 us (11%)
    pallas_call x1, Pallas kernels, fused(): pl.pallas_call(functools.partial(kernel, n), out_shape=shape, in_specs=sp...  160 us
    unnamed x72, local copies, waits for them, and re-layouts  20.2 us

profile of v1, /device:TPU:0, one launch (start us, length us, event | category | flops | bytes accessed | tf_op | source)
XLA Modules:
  0.0 182.3 jit_solution(18376956970054115153)
XLA Ops:
  0.7 0.0 copy-start.23
  0.7 0.0 copy-start.22
  0.7 0.0 copy-start.3
  0.7 0.0 copy-start.21
  0.7 0.0 copy-start.20
  0.7 0.0 copy-start.2
  0.7 0.0 copy-start.1
  0.7 0.0 copy-start
  0.7 0.0 copy-start.19
  0.7 0.0 copy-start.18
  0.8 1.2 copy.36.refs_9_
  2.0 1.1 copy.37.refs_15_
  3.1 0.0 copy-done.23
  3.1 0.0 copy-done.22
  3.1 0.0 copy-done.3
  3.1 0.0 copy-done.21
  3.2 0.0 copy-start.4
  3.2 1.0 copy-done.4
  4.2 1.0 copy-done.5
  5.1 160.1 %shard_map.313 = (bf16[4,2,96,384]{3,2,1,0:T(8,128)(2,1)S(1)}, bf16[4,2,96,384]{3,2,1,0:T(8,128)(2,1)}, bf16[4,2,96,384]{3,2,1,0:T(8,128)(2,1)}, bf16[384,768]{1...) custom-call(f32[4,2,96,384]{3,2,1,0:T(8,128)} %bitcast.48, ...), custom_call_target="tpu_custom_call" | custom-call | flops 10000000 | bytes 10000000 | tf_op jit(solution)/shard_map/pallas_call | solution.py:475
  165.3 0.7 copy-done.6
  166.0 0.7 copy-done.8
  166.7 0.7 copy-done.10
  167.4 0.7 copy-done.12
  168.1 0.7 copy-done.14
  168.9 0.7 copy-done.16
  169.6 0.6 reduce
  170.2 0.6 reduce.1
  170.8 0.9 copy.38
  171.6 0.9 copy.39
  172.5 0.8 copy.54
  173.3 0.0 copy-done.26
  173.3 0.8 copy.55
  174.1 0.0 copy-done.25
  174.1 0.8 copy.56
  175.0 0.0 copy-done.24
  175.0 0.8 copy.57
  175.8 0.7 copy.58
  176.5 0.0 copy-done.15
  176.5 0.7 copy.59
  177.2 0.7 copy.60
  177.9 0.6 copy.61
  178.5 0.6 copy.62
  179.1 0.7 copy.63
  179.8 0.7 copy.64
  180.5 0.7 copy.65
  181.2 0.6 copy.66
  181.8 0.6 copy.67
  (27 shorter events, 0.0 us)
Async XLA Ops:
  0.7 2.5 %copy-start.23 = (f32[192]{0:T(256)S(1)}, f32[192]{0:T(256)}, u32[]{:S(2)}) copy-start(f32[192]{0:T(256)} %param.35) | copy-start | bytes 2308
  0.7 2.5 %copy-start.22 = (f32[192]{0:T(256)S(1)}, f32[192]{0:T(256)}, u32[]{:S(2)}) copy-start(f32[192]{0:T(256)} %param.34) | copy-start | bytes 2308
  0.7 2.5 %copy-start.3 = (f32[192,384]{1,0:T(8,128)S(1)}, f32[192,384]{1,0:T(8,128)}, u32[]{:S(2)}) copy-start(f32[192,384]{1,0:T(8,128)} %param.30) | copy-start | bytes 884740
  0.7 2.5 %copy-start.21 = (f32[192]{0:T(256)S(1)}, f32[192]{0:T(256)}, u32[]{:S(2)}) copy-start(f32[192]{0:T(256)} %param.29) | copy-start | bytes 2308
  0.7 2.5 %copy-start.20 = (f32[192]{0:T(256)S(1)}, f32[192]{0:T(256)}, u32[]{:S(2)}) copy-start(f32[192]{0:T(256)} %param.28) | copy-start | bytes 2308
  0.7 2.5 %copy-start.2 = (f32[192,384]{1,0:T(8,128)S(1)}, f32[192,384]{1,0:T(8,128)}, u32[]{:S(2)}) copy-start(f32[192,384]{1,0:T(8,128)} %param.26) | copy-start | bytes 884740
  0.7 2.5 %copy-start.1 = (f32[192,384]{1,0:T(8,128)S(1)}, f32[192,384]{1,0:T(8,128)}, u32[]{:S(2)}) copy-start(f32[192,384]{1,0:T(8,128)} %param.25) | copy-start | bytes 884740
  0.7 2.5 %copy-start = (f32[192,384]{1,0:T(8,128)S(1)}, f32[192,384]{1,0:T(8,128)}, u32[]{:S(2)}) copy-start(f32[192,384]{1,0:T(8,128)} %param.24) | copy-start | bytes 884740
  0.7 2.5 %copy-start.19 = (f32[1,768]{1,0:T(1,128)S(1)}, f32[1,768]{1,0:T(1,128)}, u32[]{:S(2)}) copy-start(f32[1,768]{1,0:T(1,128)} %refs_5_.1) | copy-start | bytes 9220
  0.7 2.5 %copy-start.18 = (f32[1,768]{1,0:T(1,128)S(1)}, f32[1,768]{1,0:T(1,128)}, u32[]{:S(2)}) copy-start(f32[1,768]{1,0:T(1,128)} %refs_4_.1) | copy-start | bytes 9220
  3.2 1.0 copy-start.4
  4.2 1.0 copy-start.5
  165.2 0.7 copy-start.6
  166.0 0.7 copy-start.8
  166.7 0.7 copy-start.10
  167.4 0.7 copy-start.12
  168.1 0.7 copy-start.14
  168.9 0.7 copy-start.16
  170.8 2.6 %copy-start.26 = (bf16[4,2,96,384]{3,2,1,0:T(8,128)(2,1)S(1)}, bf16[4,2,96,384]{3,2,1,0:T(8,128)(2,1)}, u32[]{:S(2)}) copy-start(bf16[4,2,96,384]{3,2,1,0:T(8,128)(2,1)} %get-tuple-element.37) | copy-start | bytes 1769476
  172.5 1.6 copy-start.25
  173.3 1.6 copy-start.24
  174.1 1.6 copy-start.17
  175.0 1.5 copy-start.15
  175.0 2.3 %copy-start.13 = (f32[2,96,384]{2,1,0:T(8,128)S(1)}, f32[2,96,384]{2,1,0:T(8,128)}, u32[]{:S(2)}) copy-start(f32[2,96,384]{2,1,0:T(8,128)} %copy-done.12) | copy-start | bytes 884740
  175.8 3.3 %copy-start.11 = (f32[2,96,384]{2,1,0:T(8,128)S(1)}, f32[2,96,384]{2,1,0:T(8,128)}, u32[]{:S(2)}) copy-start(f32[2,96,384]{2,1,0:T(8,128)} %copy-done.10) | copy-start | bytes 884740
  175.8 4.0 %copy-start.9 = (f32[2,96,384]{2,1,0:T(8,128)S(1)}, f32[2,96,384]{2,1,0:T(8,128)}, u32[]{:S(2)}) copy-start(f32[2,96,384]{2,1,0:T(8,128)} %copy-done.8) | copy-start | bytes 884740
  176.5 4.0 %copy-start.7 = (f32[2,96,384]{2,1,0:T(8,128)S(1)}, f32[2,96,384]{2,1,0:T(8,128)}, u32[]{:S(2)}) copy-start(f32[2,96,384]{2,1,0:T(8,128)} %copy-done.6) | copy-start | bytes 884740

commit v2 on v1

--- a/solution.py
+++ b/solution.py
@@ -122,6 +122,8 @@
 
 MESH = pl.DeviceIdType.MESH
 HALVES = 2
+LAG = 2
+AHEAD = 4
 GAIN = 1024.0
 ORDER = (0, 3, 1, 2)
 
@@ -154,7 +156,7 @@
 def kernel(n, *refs):
     (sq, sk, sv, sm, sn, sb, pq, pk, pv, pm, pn, pb, tq, tk, tv, tm, tn, tb) = refs[:18]
     (hq, hk, hv, hm, hn, hb, xq, xk, xv, xm, xn, xb, nq, nk, nv, nm, nn, nb) = refs[18:36]
-    (X, XM, S, RL, RR, G, P_, T_, PM, TM, NX, NS, TOT, ES, ER, HM, VB, VR, NV,
+    (X, XM, S, RL, RR, G, P_, T_, NX, NS, TOT, ES, ER, HM, VB, VR, NV,
      load_sem, mix_sem, par_sem, rs_send, rl_sem, rr_sem, ag_send, ag_send2, ag_recv,
      e_send, e_recv, v_send, v_recv, out_sem, half_sem) = refs[36:]
     C, _, B, W = X.shape
@@ -165,25 +167,31 @@
     core = lax.axis_index("tp")
     rate = float(n) ** (-0.5)
     slopes = (sq, sk, sv)
-    order = [n - 1, 0] + [j for j in range(n - 2, 0, -1)]
-
-    loads = [None] * C
-    for at, m in enumerate(ORDER):
-        if m < 3:
-            for h in range(H):
-                c = at * H + h
-                loads[c] = pltpu.make_async_copy(slopes[m].at[:, h], X.at[c], load_sem.at[c])
-                loads[c].start()
-        else:
-            mix = pltpu.make_async_copy(sm, XM, mix_sem)
-            mix.start()
+
+    def rows_of(h, j=0):
+        return pl.ds(j * own + h * B, B)
+
+    loads = [[] for _ in range(C)]
     pars = []
     for at, m in enumerate(ORDER):
-        for k, (srcs, dst, odd) in enumerate((((pq, pk, pv, pm), P_, PM), ((tq, tk, tv, tm), T_, TM))):
-            d = odd if m == 3 else dst.at[pl.ds(at * H, H)]
-            cp = pltpu.make_async_copy(srcs[m], d, par_sem.at[k, m])
-            cp.start()
-            pars.append(cp)
+        for h in range(H):
+            c = at * H + h
+            if m < 3:
+                for j in range(n):
+                    loads[c].append(
+                        pltpu.make_async_copy(slopes[m].at[0, rows_of(h, j)], X.at[c, j], load_sem.at[c, j])
+                    )
+                    loads[c][-1].start()
+        if m == 3:
+            mix = pltpu.make_async_copy(sm.at[0], XM, mix_sem)
+            mix.start()
+    for at, m in enumerate(ORDER):
+        for h in range(H):
+            c = at * H + h
+            for k, (src, dst) in enumerate((((pq, pk, pv, pm)[m], P_), ((tq, tk, tv, tm)[m], T_))):
+                cp = pltpu.make_async_copy(src.at[rows_of(h)], dst.at[c], par_sem.at[k, c])
+                cp.start()
+                pars.append(cp)
 
     barrier = pltpu.get_barrier_semaphore()
     for d in range(1, n):
@@ -229,24 +237,34 @@
             device_id={"tp": 1 - core}, device_id_type=MESH,
         )
 
-    def rs(c):
-        for j in order:
-            for go, first, wait, land, send in (
-                (me < j, me == 0, rs_right, RL, rs_right),
-                (me > j, me == n - 1, rs_left, RR, rs_left),
-            ):
-                @pl.when(go)
-                def _(j=j, first=first, wait=wait, land=land, send=send):
-                    @pl.when(first)
-                    def _():
-                        S[c, j] = encode(X[c, j])
-
-                    @pl.when(jnp.logical_not(first))
-                    def _():
-                        wait(c, j).wait_recv()
-                        S[c, j] = encode(decode(land[c, j]) + X[c, j])
-
-                    send(c, j).start()
+    def first(c):
+        @pl.when(me == 0)
+        def _():
+            for j in range(n - 1, 0, -1):
+                S[c, j] = encode(X[c, j])
+                rs_right(c, j).start()
+
+        @pl.when(me == n - 1)
+        def _():
+            for j in range(n - 1):
+                S[c, j] = encode(X[c, j])
+                rs_left(c, j).start()
+
+    def plus(c):
+        for j in range(n - 1, 0, -1):
+            @pl.when(jnp.logical_and(me < j, me > 0))
+            def _(j=j):
+                rs_right(c, j).wait_recv()
+                S[c, j] = encode(decode(RL[c, j]) + X[c, j])
+                rs_right(c, j).start()
+
+    def minus(c):
+        for j in range(n - 1):
+            @pl.when(jnp.logical_and(me > j, me < n - 1))
+            def _(j=j):
+                rs_left(c, j).wait_recv()
+                S[c, j] = encode(decode(RR[c, j]) + X[c, j])
+                rs_left(c, j).start()
 
     def gather_sum(c):
         TOT[c] = X[c, me]
@@ -310,62 +328,68 @@
             for p in range(4):
                 r = b * 128 + p * 32
                 X[mixc + (r % own) // B, r // own, r % B : r % B + 32] = t[p * 32 : p * 32 + 32]
-        for src, dst in ((PM, P_), (TM, T_)):
-            t = src[...].T
-            for h in range(H):
-                dst[mixc + h] = t[h * B : h * B + B]
 
     for d in range(1, n):
         vec(d).start()
-    for c in range(C):
-        if loads[c] is not None and c < H:
-            loads[c].wait()
     VR[0] = VB[...]
     for c in range(H):
-        rs(c)
-    for c in range(C):
-        if loads[c] is not None and c >= H:
-            loads[c].wait()
+        for cp in loads[c]:
+            cp.wait()
+        first(c)
+    for c in range(H, C):
+        for cp in loads[c]:
+            cp.wait()
+    mixed_in()
+
+    for c in range(H, AHEAD):
+        first(c)
     for cp in pars:
         cp.wait()
-    mixed_in()
 
     def step(t, carry):
-        @pl.when(t < C)
-        def _():
-            rs(t)
-
-        @pl.when(jnp.logical_and(t >= 1, t <= C))
-        def _():
-            gather_sum(t - 1)
-
-        @pl.when(jnp.logical_and(t >= 2, t <= C + 1))
-        def _():
-            apply(t - 2)
-
-        @pl.when(t >= 3)
+        @pl.when(t < C - AHEAD)
+        def _():
+            first(t + AHEAD)
+
+        low = me < n // 2
+        tp_, tm_ = jnp.where(low, t, t - 1), jnp.where(low, t - 1, t)
+
+        @pl.when(jnp.logical_and(tp_ >= 0, tp_ < C))
+        def _():
+            plus(tp_)
+
+        @pl.when(jnp.logical_and(tm_ >= 0, tm_ < C))
+        def _():
+            minus(tm_)
+
+        @pl.when(jnp.logical_and(t >= LAG, t < C + LAG))
+        def _():
+            gather_sum(t - LAG)
+
+        @pl.when(jnp.logical_and(t >= LAG + 1, t < C + LAG + 1))
+        def _():
+            apply(t - LAG - 1)
+
+        @pl.when(t >= LAG + 2)
         def _():
             for j in range(1, n - 1):
                 @pl.when(passes(j))
                 def _(j=j):
-                    take(t - 3, j)
+                    take(t - LAG - 2, j)
 
         return carry
 
-    gather_sum(0)
-    lax.fori_loop(H, C + 3, step, 0)
-
-    nexts, news = (xq, xk, xv), (nq, nk, nv)
+    lax.fori_loop(0, C + LAG + 2, step, 0)
+
+    nexts, news = (xq, xk, xv, xm), (nq, nk, nv, nm)
     outs = []
     for at, m in enumerate(ORDER):
-        for k, (buf, dsts, odd, mo) in enumerate(((NX, nexts, PM, xm), (NS, news, TM, nm))):
-            if m < 3:
-                cp = pltpu.make_async_copy(buf.at[pl.ds(at * H, H)], dsts[m], out_sem.at[k, m])
-            else:
-                odd[...] = jnp.concatenate([buf[mixc + h] for h in range(H)], axis=0).T
-                cp = pltpu.make_async_copy(odd, mo, out_sem.at[k, m])
-            cp.start()
-            outs.append(cp)
+        for k, (buf, dsts) in enumerate(((NX, nexts), (NS, news))):
+            for h in range(H):
+                c = at * H + h
+                cp = pltpu.make_async_copy(buf.at[c], dsts[m].at[rows_of(h)], out_sem.at[k, c])
+                cp.start()
+                outs.append(cp)
 
     for d in range(1, n):
         vec(d).wait_send()
@@ -392,30 +416,42 @@
 
     halves = (hq, hk, hv)
 
-    def finish(c):
-        for j in range(n):
-            open_ = me != j
-            if 0 < j < n - 1:
-                open_ = jnp.logical_and(open_, jnp.logical_not(passes(j)))
-
-            @pl.when(open_)
-            def _(j=j):
-                take(c, j)
+    middle = jnp.logical_and(me > 0, me < n - 1)
+    near = jnp.where(me < n // 2, 0, n - 1)
+
+    def finish(t):
+        if t < C:
+            @pl.when(middle)
+            def _():
+                take(t, near)
+        if t >= 1:
+            @pl.when(middle)
+            def _():
+                take(t - 1, n - 1 - near)
+
+            @pl.when(jnp.logical_not(middle))
+            def _():
+                for j in range(n):
+                    @pl.when(me != j)
+                    def _(j=j):
+                        take(t - 1, j)
 
     stores = []
+    finish(0)
     for at, m in enumerate(ORDER):
         for h in range(H):
             c = at * H + h
-            finish(c)
+            finish(c + 1)
             if m < 3:
-                cp = pltpu.make_async_copy(G.at[c], halves[m].at[:, h], half_sem.at[c])
-                cp.start()
-                stores.append(cp)
+                for j in range(n):
+                    cp = pltpu.make_async_copy(G.at[c, j], halves[m].at[rows_of(h, j)], half_sem.at[c, j])
+                    cp.start()
+                    stores.append(cp)
         if m == 3:
             for j in range(n // 2):
                 rows = [G[at * H + h, 2 * j + i].astype(jnp.float32) for i in range(2) for h in range(H)]
                 HM[:, j * 2 * own : (j + 1) * 2 * own] = jnp.concatenate(rows, axis=0).T.astype(jnp.bfloat16)
-            cp = pltpu.make_async_copy(HM, hm, half_sem.at[at * H])
+            cp = pltpu.make_async_copy(HM, hm, half_sem.at[at * H, 0])
             cp.start()
             stores.append(cp)
 
@@ -453,22 +489,18 @@
     if own % (H * 32) or width % 128 or args[3].shape[1:] != (width, n * own) or args[3].shape[2] % 256:
         return shards(*args)
     C = H * 4
-    for i in range(3):
-        slopes[i] = slopes[i].reshape(n, H, B, width)
-        params[i] = params[i].reshape(H, B, width)
-        states[i] = states[i].reshape(H, B, width)
-    slopes[3] = slopes[3][0]
     for group in (params, states):
+        group[3] = group[3].T
         for i in (4, 5):
             group[i] = group[i].reshape(1, -1)
-    any_, vmem = pl.BlockSpec(memory_space=pl.ANY), pl.BlockSpec(memory_space=pltpu.VMEM)
+    any_, vmem = pl.BlockSpec(memory_space=pltpu.HBM), pl.BlockSpec(memory_space=pltpu.VMEM)
     f32, bf16 = jnp.float32, jnp.bfloat16
     specs = [any_] * 4 + [vmem] * 2
     S = jax.ShapeDtypeStruct
     rows = n * own
     shape = (
-        [S((n, H, B, width), bf16)] * 3 + [S((width, rows), bf16)] + [S((1, rows), bf16)] * 2
-        + ([S((H, B, width), f32)] * 3 + [S((width, own), f32)] + [S((1, own), f32)] * 2) * 2
+        [S((rows, width), bf16)] * 3 + [S((width, rows), bf16)] + [S((1, rows), bf16)] * 2
+        + ([S((own, width), f32)] * 4 + [S((1, own), f32)] * 2) * 2
     )
     wide = -(-own // 128) * 128
     dma = pltpu.SemaphoreType.DMA
@@ -486,8 +518,6 @@
             pltpu.VMEM((C, n, B, width), bf16),
             pltpu.VMEM((C, B, width), f32),
             pltpu.VMEM((C, B, width), f32),
-            pltpu.VMEM((width, own), f32),
-            pltpu.VMEM((width, own), f32),
             pltpu.VMEM((C, B, width), f32),
             pltpu.VMEM((C, B, width), f32),
             pltpu.VMEM((C, B, width), f32),
@@ -497,19 +527,17 @@
             pltpu.VMEM((16, wide), f32),
             pltpu.VMEM((n, 16, wide), f32),
             pltpu.VMEM((2, 2 * n, wide), f32),
-            dma((C,)), dma, dma((2, 4)), dma((C, n)), dma((C, n)), dma((C, n)), dma((C, n)), dma((C,)), dma((C, n)),
-            dma((C,)), dma((C,)), dma((n,)), dma((n,)), dma((2, 4)), dma((C,)),
+            dma((C, n)), dma, dma((2, C)), dma((C, n)), dma((C, n)), dma((C, n)), dma((C, n)), dma((C,)), dma((C, n)),
+            dma((C,)), dma((C,)), dma((n,)), dma((n,)), dma((2, C)), dma((C, n)),
         ],
         compiler_params=pltpu.CompilerParams(
-            collective_id=0, has_side_effects=True, vmem_limit_bytes=48 * 2**20
+            collective_id=0, has_side_effects=True, vmem_limit_bytes=67043328
         ),
         cost_estimate=pl.CostEstimate(flops=10**7, bytes_accessed=10**7, transcendentals=0),
     )(*slopes, *params, *states)
     outs = list(outs)
-    for i in range(3):
-        outs[i] = outs[i].reshape(rows, width)
-        for k in (6, 12):
-            outs[k + i] = outs[k + i].reshape(own, width)
+    for k in (9, 15):
+        outs[k] = outs[k].T
     for k in (4, 5, 10, 11, 16, 17):
         outs[k] = outs[k].reshape(-1)
     return tuple(outs)

time: 183 us -> 96.2 us (0.53)
  Pallas kernels: 160 us -> 80.2 us
  local copies, waits for them, and re-layouts: 20.2 us -> 12.5 us
    pallas_call x1, Pallas kernels: 160 us -> 80.2 us  [fused(): pl.pallas_call(functools.partial(kernel, n), out_shape=shape, in_specs=sp...]
    unnamed x72 -> x46, local copies, waits for them, and re-layouts: 20.2 us -> 12.5 us
where the time goes in v2:
time: 96.2 us; the launch traced here: 96 us
  Pallas kernels  80.2 us (83%)
  local copies, waits for them, and re-layouts  12.5 us (13%)
  other arithmetic  2.6 us (3%)
    pallas_call x1, Pallas kernels, fused(): pl.pallas_call(functools.partial(kernel, n), out_shape=shape, in_specs=sp...  80.2 us
    unnamed x46, local copies, waits for them, and re-layouts  12.5 us
    pallas_call x2, other arithmetic, fused(): pl.pallas_call(functools.partial(kernel, n), out_shape=shape, in_specs=sp...  2.6 us

profile of v2, /device:TPU:0, one launch (start us, length us, event | category | flops | bytes accessed | tf_op | source)
XLA Modules:
  0.0 96.0 jit_solution(13206512004714257691)
XLA Ops:
  0.7 80.2 %shard_map.313 = (bf16[768,384]{1,0:T(8,128)(2,1)}, bf16[768,384]{1,0:T(8,128)(2,1)}, bf16[768,384]{1,0:T(8,128)(2,1)}, bf16[384,768]{1,0:T(8,128)(2,1)}, bf16[1...) custom-call(f32[1,768,384]{2,1,0:T(8,128)} %refs_0_.1, ...), custom_call_target="tpu_custom_call" | custom-call | flops 10000000 | bytes 10000000 | tf_op jit(solution)/shard_map/pallas_call | solution.py:507
  80.9 0.0 copy-start.2
  80.9 1.3 %reduce = bf16[768]{0:T(1024)(128)(2,1)} reduce(bf16[1,768]{1,0:T(2,128)(2,1)} %get-tuple-element.40, bf16[]{:T(256)} %constant.6), dimensions={0}, to_apply=%get-tuple-element.40.reduce_sub_computation | reduce | bytes 3074 | tf_op jit(solution)/shard_map/pallas_call | solution.py:507
  82.2 1.3 %reduce.1 = bf16[768]{0:T(1024)(128)(2,1)} reduce(bf16[1,768]{1,0:T(2,128)(2,1)} %get-tuple-element.41, bf16[]{:T(256)} %constant.6), dimensions={0}, to_apply=%get-tuple-element.41.reduce_sub_computation | reduce | bytes 3074 | tf_op jit(solution)/shard_map/pallas_call | solution.py:507
  83.5 0.0 copy-start.1
  83.5 2.0 %copy.52 = bf16[768,384]{1,0:T(8,128)(2,1)} copy(bf16[768,384]{1,0:T(8,128)(2,1)} %get-tuple-element.72) | data formatting | bytes 1179648
  85.5 0.0 copy-done.2
  85.5 0.0 copy-start
  85.5 0.8 copy.53
  86.3 0.0 copy-done.1
  86.3 0.0 copy-start.10
  86.3 0.8 copy.54
  87.1 0.0 copy-done
  87.1 0.0 copy-start.9
  87.1 0.0 copy-start.8
  87.1 0.8 copy.55
  88.0 0.0 copy-done.10
  88.0 0.0 copy-start.7
  88.0 0.0 copy-start.14
  88.0 0.0 copy-start.6
  88.0 0.7 copy.56
  88.7 0.0 copy-done.9
  88.7 0.0 copy-start.5
  88.7 0.7 copy.57
  89.4 0.0 copy-done.8
  89.4 0.0 copy-start.4
  89.4 0.7 copy.58
  90.1 0.0 copy-done.7
  90.1 0.0 copy-start.3
  90.1 0.7 copy.59
  90.9 0.0 copy-done.14
  90.9 0.6 copy.60
  91.4 0.0 copy-done.13
  91.4 0.6 copy.61
  92.0 0.0 copy-done.6
  92.0 0.0 copy-start.12
  92.0 0.0 copy-start.11
  92.0 0.7 copy.62
  92.7 0.0 copy-done.5
  92.7 0.7 copy.63
  93.4 0.0 copy-done.4
  93.4 0.7 copy.64
  94.1 0.0 copy-done.3
  94.1 0.7 copy.65
  94.9 0.0 copy-done.12
  94.9 0.6 copy.66
  95.4 0.0 copy-done.11
  95.4 0.6 copy.67
  (1 shorter events, 0.0 us)
Async XLA Ops:
  80.9 4.6 %copy-start.2 = (bf16[768,384]{1,0:T(8,128)(2,1)S(1)}, bf16[768,384]{1,0:T(8,128)(2,1)}, u32[]{:S(2)}) copy-start(bf16[768,384]{1,0:T(8,128)(2,1)} %get-tuple-element.73) | copy-start | bytes 1769476
  83.5 2.8 %copy-start.1 = (bf16[768,384]{1,0:T(8,128)(2,1)S(1)}, bf16[768,384]{1,0:T(8,128)(2,1)}, u32[]{:S(2)}) copy-start(bf16[768,384]{1,0:T(8,128)(2,1)} %get-tuple-element.74) | copy-start | bytes 1769476
  85.5 1.6 %copy-start = (bf16[384,768]{1,0:T(8,128)(2,1)S(1)}, bf16[384,768]{1,0:T(8,128)(2,1)}, u32[]{:S(2)}) copy-start(bf16[384,768]{1,0:T(8,128)(2,1)} %get-tuple-element.75) | copy-start | bytes 1769476
  86.3 1.6 %copy-start.10 = (f32[192,384]{1,0:T(8,128)S(1)}, f32[192,384]{1,0:T(8,128)}, u32[]{:S(2)}) copy-start(f32[192,384]{1,0:T(8,128)} %get-tuple-element.78) | copy-start | bytes 884740
  87.1 1.6 %copy-start.9 = (f32[192,384]{1,0:T(8,128)S(1)}, f32[192,384]{1,0:T(8,128)}, u32[]{:S(2)}) copy-start(f32[192,384]{1,0:T(8,128)} %get-tuple-element.79) | copy-start | bytes 884740
  87.1 2.3 %copy-start.8 = (f32[192,384]{1,0:T(8,128)S(1)}, f32[192,384]{1,0:T(8,128)}, u32[]{:S(2)}) copy-start(f32[192,384]{1,0:T(8,128)} %get-tuple-element.80) | copy-start | bytes 884740
  88.0 2.2 %copy-start.7 = (f32[192,384]{1,0:T(8,128)S(1)}, f32[192,384]{1,0:T(8,128)}, u32[]{:S(2)}) copy-start(f32[192,384]{1,0:T(8,128)} %get-tuple-element.45) | copy-start | bytes 884740
  88.0 2.9 %copy-start.14 = (f32[1,192]{1,0:T(1,128)S(1)}, f32[1,192]{1,0:T(1,128)}, u32[]{:S(2)}) copy-start(f32[1,192]{1,0:T(1,128)} %get-tuple-element.46) | copy-start | bytes 2308
  88.0 3.5 %copy-start.13 = (f32[1,192]{1,0:T(1,128)S(1)}, f32[1,192]{1,0:T(1,128)}, u32[]{:S(2)}) copy-start(f32[1,192]{1,0:T(1,128)} %get-tuple-element.47) | copy-start | bytes 2308
  88.0 4.0 %copy-start.6 = (f32[192,384]{1,0:T(8,128)S(1)}, f32[192,384]{1,0:T(8,128)}, u32[]{:S(2)}) copy-start(f32[192,384]{1,0:T(8,128)} %get-tuple-element.84) | copy-start | bytes 884740
  88.7 4.0 %copy-start.5 = (f32[192,384]{1,0:T(8,128)S(1)}, f32[192,384]{1,0:T(8,128)}, u32[]{:S(2)}) copy-start(f32[192,384]{1,0:T(8,128)} %get-tuple-element.85) | copy-start | bytes 884740
  89.4 4.0 %copy-start.4 = (f32[192,384]{1,0:T(8,128)S(1)}, f32[192,384]{1,0:T(8,128)}, u32[]{:S(2)}) copy-start(f32[192,384]{1,0:T(8,128)} %get-tuple-element.86) | copy-start | bytes 884740
  90.1 4.0 %copy-start.3 = (f32[192,384]{1,0:T(8,128)S(1)}, f32[192,384]{1,0:T(8,128)}, u32[]{:S(2)}) copy-start(f32[192,384]{1,0:T(8,128)} %get-tuple-element.51) | copy-start | bytes 884740
  92.0 2.9 %copy-start.12 = (f32[1,192]{1,0:T(1,128)S(1)}, f32[1,192]{1,0:T(1,128)}, u32[]{:S(2)}) copy-start(f32[1,192]{1,0:T(1,128)} %get-tuple-element.52) | copy-start | bytes 2308
  92.0 3.4 %copy-start.11 = (f32[1,192]{1,0:T(1,128)S(1)}, f32[1,192]{1,0:T(1,128)}, u32[]{:S(2)}) copy-start(f32[1,192]{1,0:T(1,128)} %get-tuple-element.53) | copy-start | bytes 2308

commit v3 on v2

--- a/solution.py
+++ b/solution.py
@@ -478,6 +478,20 @@
 
     lax.fori_loop(0, C, drain, 0)
     for cp in outs + stores:
+        cp.wait()
+
+
+def settle(count, *refs):
+    src, dst, mid = refs[:count], refs[count : 2 * count], refs[2 * count : 3 * count]
+    got, put = refs[3 * count :]
+    ins = [pltpu.make_async_copy(src[i], mid[i], got.at[i]) for i in range(count)]
+    outs = [pltpu.make_async_copy(mid[i], dst[i], put.at[i]) for i in range(count)]
+    for cp in ins:
+        cp.start()
+    for a, b in zip(ins, outs):
+        a.wait()
+        b.start()
+    for cp in outs:
         cp.wait()
 
 
@@ -535,7 +549,18 @@
         ),
         cost_estimate=pl.CostEstimate(flops=10**7, bytes_accessed=10**7, transcendentals=0),
     )(*slopes, *params, *states)
-    outs = list(outs)
+    count = len(shape)
+    outs = list(
+        pl.pallas_call(
+            functools.partial(settle, count),
+            out_shape=shape,
+            in_specs=[any_] * count,
+            out_specs=[any_] * count,
+            scratch_shapes=[pltpu.VMEM(s.shape, s.dtype) for s in shape] + [dma((count,)), dma((count,))],
+            compiler_params=pltpu.CompilerParams(vmem_limit_bytes=67043328),
+            cost_estimate=pl.CostEstimate(flops=10**6, bytes_accessed=10**7, transcendentals=0),
+        )(*outs)
+    )
     for k in (9, 15):
         outs[k] = outs[k].T
     for k in (4, 5, 10, 11, 16, 17):

time: 96.2 us -> 88 us (0.915)
  local copies, waits for them, and re-layouts: 12.5 us -> 0 us
  Pallas kernels: 80.2 us -> 84.5 us
    unnamed x46 -> x0, local copies, waits for them, and re-layouts: 12.5 us -> none
    pallas_call x0 -> x1, Pallas kernels: none -> 4.26 us  [fused(): pl.pallas_call(functools.partial(settle, count), out_shape=shape, in_spec...]
where the time goes in v3:
time: 88 us; the launch traced here: 87.7 us
  Pallas kernels  84.5 us (96%)
  other arithmetic  2.54 us (3%)
    pallas_call x1, Pallas kernels, fused(): pl.pallas_call(functools.partial(kernel, n), out_shape=shape, in_specs=sp...  80.2 us
    pallas_call x1, Pallas kernels, fused(): pl.pallas_call(functools.partial(settle, count), out_shape=shape, in_spec...  4.26 us
    pallas_call x2, other arithmetic, fused(): pl.pallas_call(functools.partial(settle, count), out_shape=shape, in_spec...  2.54 us

profile of v3, /device:TPU:0, one launch (start us, length us, event | category | flops | bytes accessed | tf_op | source)
XLA Modules:
  0.0 87.7 jit_solution(9459905810881773584)
XLA Ops:
  0.7 80.2 %shard_map.313 = (bf16[768,384]{1,0:T(8,128)(2,1)}, bf16[768,384]{1,0:T(8,128)(2,1)}, bf16[768,384]{1,0:T(8,128)(2,1)}, bf16[384,768]{1,0:T(8,128)(2,1)}, bf16[1...) custom-call(f32[1,768,384]{2,1,0:T(8,128)} %refs_0_.1, ...), custom_call_target="tpu_custom_call" | custom-call | flops 10000000 | bytes 10000000 | tf_op jit(solution)/shard_map/pallas_call | solution.py:521
  80.9 4.3 %shard_map.314 = (bf16[768,384]{1,0:T(8,128)(2,1)}, bf16[768,384]{1,0:T(8,128)(2,1)}, bf16[768,384]{1,0:T(8,128)(2,1)}, bf16[384,768]{1,0:T(8,128)(2,1)}, bf16[1...) custom-call(bf16[768,384]{1,0:T(8,128)(2,1)} %get-tuple-element.54.r, ...), custom_call_target="tpu_custom_call" | custom-call | flops 1000000 | bytes 10000000 | tf_op jit(solution)/shard_map/pallas_call | solution.py:554
  85.2 1.3 %reduce = bf16[768]{0:T(1024)(128)(2,1)} reduce(bf16[1,768]{1,0:T(2,128)(2,1)} %get-tuple-element.76, bf16[]{:T(256)} %constant.6), dimensions={0}, to_apply=%get-tuple-element.76.reduce_sub_computation | reduce | bytes 3074 | tf_op jit(solution)/shard_map/pallas_call | solution.py:554
  86.4 1.3 %reduce.1 = bf16[768]{0:T(1024)(128)(2,1)} reduce(bf16[1,768]{1,0:T(2,128)(2,1)} %get-tuple-element.77, bf16[]{:T(256)} %constant.6), dimensions={0}, to_apply=%get-tuple-element.77.reduce_sub_computation | reduce | bytes 3074 | tf_op jit(solution)/shard_map/pallas_call | solution.py:554
